TPU v7x, 32 devices: a whole 2x2x4 slice. The times are simulated.
32 devices in a mesh: pipe: 4 (over z), dp: 4 (over x, core), expert: 2 (over y).
Axes of the slice: x: 2, y: 2, z: 4, core: 2. Of those that a mesh axis runs over, the one named last changes fastest.
Arguments:
- entering: bfloat16 [4, 512, 4096], P('pipe', 'dp', 'expert'), may hold values from -6 to 6
- pending: bfloat16 [4, 512, 4096], P('pipe', 'dp', 'expert'), may hold values from -6 to 6
- stashed_in: bfloat16 [4, 512, 4096], P('pipe', 'dp', 'expert'), may hold values from -6 to 6
- forward_routes: int32 [4, 512, 2], P('pipe', 'dp'), may hold values from 0 to 3, all different within a row; in each aligned block of 128 rows (0 to 127, 128 to 255, ..., all dimensions but the last counted through in order) at most 64 rows name the same one
- backward_routes: int32 [4, 512, 2], P('pipe', 'dp'), may hold values from 0 to 3, all different within a row; in each aligned block of 128 rows (0 to 127, 128 to 255, ..., all dimensions but the last counted through in order) at most 64 rows name the same one
- norm_gains: float32 [4, 4096], P('pipe', 'expert'), may hold values from 0.5 to 1.5
- w_router: bfloat16 [4, 4096, 4], P('pipe', 'expert'), may hold values from -0.09375 to 0.09375
- w_gateup: bfloat16 [4, 4, 4096, 2, 1024], P('pipe', 'dp', None, None, 'expert'), may hold values from -0.09375 to 0.09375
- w_down: bfloat16 [4, 4, 1024, 4096], P('pipe', 'dp', 'expert'), may hold values from -0.1875 to 0.1875
Outputs:
- forward_out: bfloat16 [4, 512, 4096], P('pipe', 'dp', 'expert')
- input_grads: bfloat16 [4, 512, 4096], P('pipe', 'dp', 'expert')
- passed_forward: bfloat16 [4, 512, 4096], P('pipe', 'dp', 'expert')
- passed_backward: bfloat16 [4, 512, 4096], P('pipe', 'dp', 'expert')
- gain_grads: float32 [4, 4096], P('pipe', 'expert')
Inputs may be any that keep to these rules, and one draw needn't show every extreme that they name: `forward_routes`: each row names 2 different experts; in each aligned block of 128 rows (one sequence) every expert is named by exactly 64 rows. `backward_routes`: each row names 2 different experts; in each aligned block of 128 rows (one sequence) every expert is named by exactly 64 rows.
All inputs are finite; a program needn't handle non-finite values.
Results may differ from a plain program's by a relative error of at most 0.015.
Values may be sent and summed in bfloat16 or wider, within the bound.
A program may use at most 64 MiB of HBM per device.

v0:
```python
import jax
import jax.numpy as jnp
from jax import lax
from jax.sharding import PartitionSpec as P

D = 4096
ROUTE_SCALE = 2.827
EPSILON = 1e-05


def shifted(block, axis, distance):
    devices = range(lax.axis_size(axis))
    route = [(i - distance, i) for i in devices if i - distance in devices]
    return lax.ppermute(block, axis, route)


def feature_sum(values):
    return lax.psum(values, "expert")


def normalize(tokens, gain_row):
    values = tokens.astype(jnp.float32)
    squares = feature_sum(jnp.sum(values * values, axis=-1, keepdims=True))
    scaling = lax.rsqrt(squares / D + EPSILON)
    return (values, scaling, (values * scaling * gain_row).astype(jnp.bfloat16))


def gating(moe_in, router, routes):
    experts = router.shape[1]
    logits = feature_sum(jnp.dot(moe_in, router, preferred_element_type=jnp.float32))
    selection = (routes[:, :, None] == jnp.arange(experts, dtype=jnp.int32)[None, None, :]).astype(
        jnp.float32
    )
    chosen = jnp.sum(logits[:, None, :] * selection, axis=-1)
    lifted = jax.nn.sigmoid(chosen)
    lifted_sum = jnp.sum(lifted, axis=-1, keepdims=True)
    return (ROUTE_SCALE * lifted / lifted_sum, lifted, lifted_sum, selection)


def layout(routes, experts):
    capacity = routes.shape[0] * routes.shape[1] // experts
    flattened = routes.reshape(-1)
    member = (flattened[:, None] == jnp.arange(experts, dtype=jnp.int32)[None, :]).astype(jnp.int32)
    before = jnp.cumsum(member, axis=0) - member
    position = jnp.sum(before * member, axis=1)
    destination = flattened * capacity + position
    placing = (
        destination[:, None] == jnp.arange(experts * capacity, dtype=jnp.int32)[None, :]
    ).astype(jnp.bfloat16)
    return (capacity, destination, placing)


def spread(placing, route_rows):
    return jnp.einsum("rc,rd->cd", placing, route_rows, preferred_element_type=jnp.float32).astype(
        jnp.bfloat16
    )


def add_projection(gate_up, segment):
    return jnp.einsum("sxcd,xdkf->sxckf", segment, gate_up, preferred_element_type=jnp.float32)


def run_forward(tokens, routes, gain_row, router, gate_up, down_w):
    length, local_width = tokens.shape
    experts = router.shape[1]
    local_count = gate_up.shape[0]
    values, scaling, moe_in = normalize(tokens, gain_row)
    gate_weights, lifted, lifted_sum, selection = gating(moe_in, router, routes)
    capacity, destination, placing = layout(routes, experts)
    route_rows = jnp.repeat(moe_in, routes.shape[1], axis=0)
    buffer = spread(placing, route_rows).reshape(
        experts // local_count, local_count, capacity, local_width
    )

    def compute(received):
        projected = add_projection(gate_up, lax.all_gather(received, "expert", axis=3, tiled=True))
        gate_pre = projected[:, :, :, 0]
        second = projected[:, :, :, 1]
        inner_act = (jax.nn.silu(gate_pre) * second).astype(jnp.bfloat16)
        partial_value = jnp.einsum(
            "sxcf,xfd->sxcd", inner_act, down_w, preferred_element_type=jnp.float32
        )
        summed = lax.psum_scatter(
            partial_value.astype(jnp.bfloat16), "expert", scatter_dimension=3, tiled=True
        )
        return lax.all_to_all(summed, "dp", split_axis=0, concat_axis=0, tiled=True)

    results = compute(lax.all_to_all(buffer, "dp", split_axis=0, concat_axis=0, tiled=True))
    picked = jnp.take(
        results.reshape(experts * capacity, local_width), destination, axis=0
    ).reshape(length, routes.shape[1], local_width)
    return (values + jnp.sum(gate_weights[:, :, None] * picked.astype(jnp.float32), axis=1)).astype(
        jnp.bfloat16
    )


def run_backward(stashed, incoming, routes, gain_row, router, gate_up, down_w):
    length, local_width = stashed.shape
    experts = router.shape[1]
    local_count = gate_up.shape[0]
    chosen_count = routes.shape[1]
    values, scaling, moe_in = normalize(stashed, gain_row)
    gate_weights, lifted, lifted_sum, selection = gating(moe_in, router, routes)
    capacity, destination, placing = layout(routes, experts)
    slot_shape = (experts // local_count, local_count, capacity, local_width)
    row_buffer = spread(placing, jnp.repeat(moe_in, chosen_count, axis=0)).reshape(slot_shape)
    upstream_buffer = spread(placing, jnp.repeat(incoming, chosen_count, axis=0)).reshape(
        slot_shape
    )

    def compute(received):
        rows_in, up_in = received
        rows_piece = lax.all_gather(rows_in, "expert", axis=3, tiled=True)
        up_piece = lax.all_gather(up_in, "expert", axis=3, tiled=True)
        first_sum = jnp.einsum(
            "sxcd,xdkf->sxckf", rows_piece, gate_up, preferred_element_type=jnp.float32
        )
        second_sum = jnp.einsum(
            "sxcd,xfd->sxcf", up_piece, down_w, preferred_element_type=jnp.float32
        )
        gate_pre = first_sum[:, :, :, 0]
        second = first_sum[:, :, :, 1]
        lifted_act = jax.nn.sigmoid(gate_pre)
        activated = gate_pre * lifted_act
        inner_act = (activated * second).astype(jnp.bfloat16)
        gate_total = feature_sum(
            jnp.sum(inner_act.astype(jnp.float32) * second_sum, axis=-1)
        ).astype(jnp.bfloat16)
        grad_first = (
            second_sum * second * lifted_act * (1.0 + gate_pre * (1.0 - lifted_act))
        ).astype(jnp.bfloat16)
        grad_second = (second_sum * activated).astype(jnp.bfloat16)
        stacked = jnp.stack([grad_first, grad_second], axis=3)
        partial_value = jnp.einsum(
            "sxckf,xdkf->sxcd", stacked, gate_up, preferred_element_type=jnp.float32
        )
        summed = lax.psum_scatter(
            partial_value.astype(jnp.bfloat16), "expert", scatter_dimension=3, tiled=True
        )
        return (
            lax.all_to_all(summed, "dp", split_axis=0, concat_axis=0, tiled=True),
            lax.all_to_all(gate_total, "dp", split_axis=0, concat_axis=0, tiled=True),
        )

    back_rows, back_gate = compute(
        (
            lax.all_to_all(row_buffer, "dp", split_axis=0, concat_axis=0, tiled=True),
            lax.all_to_all(upstream_buffer, "dp", split_axis=0, concat_axis=0, tiled=True),
        )
    )
    back_rows = jnp.take(
        back_rows.reshape(experts * capacity, local_width), destination, axis=0
    ).reshape(length, chosen_count, local_width)
    back_gate = (
        jnp.take(back_gate.reshape(-1), destination, axis=0)
        .reshape(length, chosen_count)
        .astype(jnp.float32)
    )
    moe_cot = jnp.sum(gate_weights[:, :, None] * back_rows.astype(jnp.float32), axis=1).astype(
        jnp.bfloat16
    )
    mixed = jnp.sum(back_gate * lifted, axis=-1, keepdims=True) / lifted_sum
    chosen_cot = ROUTE_SCALE * (back_gate - mixed) / lifted_sum * lifted * (1.0 - lifted)
    logit_cot = jnp.sum(chosen_cot[:, :, None] * selection, axis=1)
    norm_cot = moe_cot.astype(jnp.float32) + jnp.dot(
        logit_cot, router.astype(jnp.float32).T, precision=lax.Precision.HIGHEST
    )
    scaled = norm_cot * gain_row
    inner_product = feature_sum(jnp.sum(scaled * values, axis=-1, keepdims=True))
    token_cot = (
        incoming.astype(jnp.float32)
        + scaling * scaled
        - values * (scaling * scaling * scaling) * inner_product / D
    )
    gain_cot = jnp.sum(norm_cot * values * scaling, axis=0)
    return (token_cot.astype(jnp.bfloat16), gain_cot)


def local(
    entering,
    pending,
    stashed_in,
    forward_routes,
    backward_routes,
    norm_gains,
    w_router,
    w_gateup,
    w_down,
):
    gain_row = norm_gains[0]
    router = w_router[0]
    gate_up = w_gateup[0]
    down_w = w_down[0]
    produced = run_forward(entering[0], forward_routes[0], gain_row, router, gate_up, down_w)
    cotangent, gain_part = run_backward(
        stashed_in[0], pending[0], backward_routes[0], gain_row, router, gate_up, down_w
    )
    passed_forward = shifted(produced, "pipe", 1)
    passed_backward = shifted(cotangent, "pipe", -1)
    gain_total = lax.psum(gain_part, "dp")
    return (
        produced[None],
        cotangent[None],
        passed_forward[None],
        passed_backward[None],
        gain_total[None],
    )


def solution(mesh):
    placed = (
        P("pipe", "dp", "expert"),
        P("pipe", "dp", "expert"),
        P("pipe", "dp", "expert"),
        P("pipe", "dp", None),
        P("pipe", "dp", None),
        P("pipe", "expert"),
        P("pipe", "expert", None),
        P("pipe", "dp", None, None, "expert"),
        P("pipe", "dp", "expert", None),
    )
    return jax.shard_map(
        local,
        mesh=mesh,
        in_specs=placed,
        out_specs=(
            P("pipe", "dp", "expert"),
            P("pipe", "dp", "expert"),
            P("pipe", "dp", "expert"),
            P("pipe", "dp", "expert"),
            P("pipe", "expert"),
        ),
        check_vma=False,
    )
```

profile of v0, /device:TPU:0, one launch (start us, length us, event | category | flops | bytes accessed | tf_op | source)
XLA Modules:
  0.0 331.1 jit_solution(16429123784945353185)
XLA Ops:
  7.2 0.8 copy.106
  8.2 0.1 reshape_squeeze.7
  8.3 1.2 fusion.46
  9.5 5.9 %psum.51 = f32[128,1]{0,1:T(1,128)S(1)} all-reduce(f32[128,1]{0,1:T(1,128)S(1)} %bitcast.284), channel_id=1, replica_groups=mesh['pipe'=4,'dp'=4,'expert'=2] {'expert'}, use_global_device_ids=true, to_apply=%region_11.13 | all-reduce | flops 128 | bytes 1024 | tf_op jit(solution)/shard_map/psum | solution.py:18
  15.4 1.2 fusion.48
  16.7 0.6 broadcast_in_dim.66
  17.3 0.4 reshape.435
  17.8 1.2 reduce-window.16
  19.4 0.6 convolution_convert_fusion.1
  20.0 17.7 %all_to_all.30 = bf16[4,1,64,2048]{3,2,1,0:T(8,128)(2,1)} all-to-all(bf16[4,1,64,2048]{3,2,1,0:T(8,128)(2,1)S(1)} %bitcast.261), channel_id=1, replica_groups=mesh['pipe'=4,'dp'=4,'expert'=2] {'dp'}, dimensions={0} | all-to-all | bytes 2097152 | tf_op jit(solution)/shard_map/all_to_all | solution.py:147
  37.8 0.6 broadcast_in_dim.65
  38.5 0.4 reshape.432
  38.9 0.6 convolution_convert_fusion.2
  39.5 17.6 %all_to_all.31 = bf16[4,1,64,2048]{3,2,1,0:T(8,128)(2,1)} all-to-all(bf16[4,1,64,2048]{3,2,1,0:T(8,128)(2,1)S(1)} %bitcast.262), channel_id=1, replica_groups=mesh['pipe'=4,'dp'=4,'expert'=2] {'dp'}, dimensions={0} | all-to-all | bytes 2097152 | tf_op jit(solution)/shard_map/all_to_all | solution.py:148
  57.1 14.7 %all-gather.8.cloned.1.call-done = bf16[4,1,64,4096]{3,2,0,1:T(8,128)(2,1)} async-done(((bf16[4,1,64,2048]{3,2,0,1:T(8,128)(2,1)}), bf16[4,1,64,4096]{3,2,0,1:T(8,128)(2,1)}) %all-gather.8.cloned.1.call-update) | async-done | bytes 2097168 | tf_op jit(solution)/shard_map/all_gather | solution.py:113
  71.8 6.3 %fusion.26 = f32[4,1,64,2,512]{4,2,0,3,1:T(8,128)S(1)} fusion(bf16[4096,2,512,1]{2,1,0,3:T(2,128)(2,1)} %bitcast.285, bf16[4,1,64,4096]{3,2,0,1:T(8,128)(2,1)} %all-gather.8.cloned.1.call-done), kind=kOutput, calls=%fused_computation.33 | convolution fusion | flops 2147483648 | bytes 11534336 | tf_op jit(solution)/shard_map/sxcd,xdkf->sxckf/dot_general | solution.py:115
  78.1 28.3 %all-gather.6.cloned.1.call-done = bf16[4,1,64,4096]{3,2,0,1:T(8,128)(2,1)} async-done(((bf16[4,1,64,2048]{3,2,0,1:T(8,128)(2,1)}), bf16[4,1,64,4096]{3,2,0,1:T(8,128)(2,1)}) %all-gather.6.cloned.1.call-update) | async-done | bytes 2097168 | tf_op jit(solution)/shard_map/all_gather | solution.py:114
  106.5 4.4 %fusion.82 = (bf16[4,1,64,1,512]{4,2,0,3,1:T(8,128)(2,1)S(1)}, f32[4,64]{1,0:T(4,128)S(1)}, bf16[4,1,64,1,512]{4,2,0,3,1:T(8,128)(2,1)S(1)}) fusion(f32[4,1,64,2,512]{4,2,0,3,1:T(8,128)S(1)} %fusion.26, bf16[1,1,512,4096]{3,2,1,0:T(8,128)(2,1)} %param.19, bf16[4,1,64,4096]{3,2,0,1:T(8,128)(2,1)} %all-gather.6.cloned.1.call-done), kind=kOutput, calls=%fused_computation.89 | convolution fusion | flops 1076100864 | bytes 7865344 | tf_op jit(solution)/shard_map/sxcd,xfd->sxcf/dot_general | solution.py:118
  110.8 7.1 %fusion.14 = bf16[4,1,64,4096]{3,2,0,1:T(8,128)(2,1)} fusion(bf16[4096,2,512,1]{2,1,0,3:T(2,128)(2,1)} %bitcast.286, bf16[4,1,64,1,512]{4,2,0,3,1:T(8,128)(2,1)S(1)} %get-tuple-element.25, bf16[4,1,64,1,512]{4,2,0,3,1:T(8,128)(2,1)S(1)} %get-tuple-element.23), kind=kOutput, calls=%fused_computation.14 | convolution fusion | flops 2148794368 | bytes 11010048 | tf_op jit(solution)/shard_map/sxckf,xdkf->sxcd/dot_general | solution.py:134
  118.1 0.5 copy-done.8
  118.7 0.1 eq.109
  118.9 0.1 reshape_squeeze.6
  119.2 0.1 mul.340
  119.4 1.2 reduce-window.14
  121.1 0.2 fusion.58
  121.3 0.3 fusion.69
  121.6 8.1 %all-reduce.1 = (f32[128,1]{0,1:T(1,128)S(1)}, f32[128,4]{0,1:T(4,128)S(1)}, bf16[4,1,64]{2,1,0:T(2,128)(2,1)}) all-reduce(f32[128,1]{0,1:T(1,128)S(1)} %bitcast.282, f32[128,4]{0,1:T(4,128)S(1)} %fusion.69, f32[4,1,64]{2,1,0:T(1,128)S(1)} %bitcast.283), channel_id=1, replica_groups=mesh['pipe'=4,'dp'=4,'expert'=2] {'expert'}, use_global_device_ids=true, to_apply=%region_1.0 | all-reduce | flops 896 | bytes 6656 | tf_op jit(solution)/shard_map/psum | solution.py:18
  129.7 3.2 all-to-all-start.5
  132.9 3.6 %all-to-all-done.5 = bf16[4,1,64]{2,1,0:T(2,128)(2,1)S(1)} async-done(((bf16[4,1,64]{2,1,0:T(2,128)(2,1)}), bf16[4,1,64]{2,1,0:T(2,128)(2,1)S(1)}, u32[]{:S(2)}, u32[]{:S(2)}) %all-to-all-start.5) | async-done | bytes 544 | tf_op jit(solution)/shard_map/all_to_all | solution.py:142
  136.6 13.9 %reduce-scatter.5.cloned.1.call-done = bf16[4,1,64,2048]{3,2,0,1:T(8,128)(2,1)} async-done(((bf16[4,1,64,4096]{3,2,0,1:T(8,128)(2,1)}), bf16[4,1,64,2048]{3,2,0,1:T(8,128)(2,1)}) %reduce-scatter.5.cloned.1.call-update) | async-done | bytes 1048592 | tf_op jit(solution)/shard_map/reduce_scatter | solution.py:137
  150.5 3.5 %all-to-all-start.4 = ((bf16[4,1,64,2048]{3,2,1,0:T(8,128)(2,1)}), bf16[4,1,64,2048]{3,2,1,0:T(8,128)(2,1)S(1)}, u32[]{:S(2)}, u32[]{:S(2)}) async-start(bf16[4,1,64,2048]{3,2,1,0:T(8,128)(2,1)} %bitcast.265), calls=%async_computation.6 | async-start | bytes 2097152 | tf_op jit(solution)/shard_map/all_to_all | solution.py:141
  154.0 0.2 all-gather.4.cloned.1.call-start
  154.2 0.3 fusion.66
  154.6 1.9 gather_fusion
  156.5 0.2 gather.10
  157.0 11.4 %all-to-all-done.4 = bf16[4,1,64,2048]{3,2,1,0:T(8,128)(2,1)S(1)} async-done(((bf16[4,1,64,2048]{3,2,1,0:T(8,128)(2,1)}), bf16[4,1,64,2048]{3,2,1,0:T(8,128)(2,1)S(1)}, u32[]{:S(2)}, u32[]{:S(2)}) %all-to-all-start.4) | async-done | bytes 1048608 | tf_op jit(solution)/shard_map/all_to_all | solution.py:141
  168.4 2.3 gather_fusion.2
  170.7 1.4 select_convert_fusion
  172.2 2.3 reshape.445
  174.5 4.8 %multiply_reduce_fusion = bf16[128,2048]{1,0:T(8,128)(2,1)S(1)} fusion(f32[128,2,2048]{2,1,0:T(2,128)} %reshape.445, f32[128,2]{1,0:T(8,128)S(1)} %copy.105), kind=kLoop, calls=%fused_computation.25 | loop fusion | flops 786432 | bytes 2622464 | tf_op jit(solution)/shard_map/reduce_sum | solution.py:159
  179.3 1.0 fusion.55
  180.3 4.9 %all-reduce = (f32[128,4]{0,1:T(4,128)S(1)}, f32[128]{0:T(128)S(1)}) all-reduce(f32[128,4]{0,1:T(4,128)S(1)} %fusion.66, f32[128]{0:T(128)S(1)} %get-tuple-element.7), channel_id=1, replica_groups=mesh['pipe'=4,'dp'=4,'expert'=2] {'expert'}, use_global_device_ids=true, to_apply=%region_2.0 | all-reduce | flops 640 | bytes 5120 | tf_op jit(solution)/shard_map/psum | solution.py:18
  185.2 0.5 fusion.52
  185.8 0.6 broadcast_in_dim.36
  186.4 0.4 reshape.425
  186.8 0.6 convolution_convert_fusion.3
  187.4 17.6 %all_to_all.32 = bf16[4,1,64,2048]{3,2,1,0:T(8,128)(2,1)} all-to-all(bf16[4,1,64,2048]{3,2,1,0:T(8,128)(2,1)S(1)} %bitcast.263), channel_id=1, replica_groups=mesh['pipe'=4,'dp'=4,'expert'=2] {'dp'}, dimensions={0} | all-to-all | bytes 2097152 | tf_op jit(solution)/shard_map/all_to_all | solution.py:88
  205.1 32.3 %all-gather.4.cloned.1.call-done = bf16[4,1,64,4096]{3,2,0,1:T(8,128)(2,1)} async-done(((bf16[4,1,64,2048]{3,2,0,1:T(8,128)(2,1)}), bf16[4,1,64,4096]{3,2,0,1:T(8,128)(2,1)}) %all-gather.4.cloned.1.call-update) | async-done | bytes 2097168 | tf_op jit(solution)/shard_map/all_gather | solution.py:76
  237.4 6.5 %fusion.31 = f32[4,1,64,2,512]{4,2,3,0,1:T(8,128)S(1)} fusion(bf16[4096,2,512]{2,1,0:T(2,128)(2,1)} %bitcast.287, bf16[4,1,64,4096]{3,2,0,1:T(8,128)(2,1)} %all-gather.4.cloned.1.call-done), kind=kOutput, calls=%fused_computation.34 | convolution fusion | flops 2147483648 | bytes 11534336 | tf_op jit(solution)/shard_map/sxcd,xdkf->sxckf/dot_general | solution.py:60
  243.9 2.7 fusion.13
  246.6 32.1 %reduce-scatter.3.cloned.1.call-done = bf16[4,1,64,2048]{3,2,0,1:T(8,128)(2,1)} async-done(((bf16[4,1,64,4096]{3,2,0,1:T(8,128)(2,1)}), bf16[4,1,64,2048]{3,2,0,1:T(8,128)(2,1)}) %reduce-scatter.3.cloned.1.call-update) | async-done | bytes 1048592 | tf_op jit(solution)/shard_map/reduce_scatter | solution.py:83
  278.6 3.5 %all-to-all-start.1 = ((bf16[4,1,64,2048]{3,2,1,0:T(8,128)(2,1)}), bf16[4,1,64,2048]{3,2,1,0:T(8,128)(2,1)S(1)}, u32[]{:S(2)}, u32[]{:S(2)}) async-start(bf16[4,1,64,2048]{3,2,1,0:T(8,128)(2,1)} %bitcast.266), calls=%async_computation.2 | async-start | bytes 2097152 | tf_op jit(solution)/shard_map/all_to_all | solution.py:86
  282.4 1.5 collective-permute-start.1
  283.9 12.7 %all-to-all-done.1 = bf16[4,1,64,2048]{3,2,1,0:T(8,128)(2,1)S(1)} async-done(((bf16[4,1,64,2048]{3,2,1,0:T(8,128)(2,1)}), bf16[4,1,64,2048]{3,2,1,0:T(8,128)(2,1)S(1)}, u32[]{:S(2)}, u32[]{:S(2)}) %all-to-all-start.1) | async-done | bytes 1048608 | tf_op jit(solution)/shard_map/all_to_all | solution.py:86
  296.5 2.3 gather_fusion.1
  298.9 1.4 select_convert_fusion.1
  300.3 2.3 reshape.443
  302.6 4.7 %multiply_reduce_fusion.1 = f32[128,2048]{1,0:T(8,128)S(1)} fusion(f32[128,2,2048]{2,1,0:T(2,128)} %reshape.443, f32[128,2]{1,0:T(8,128)S(1)} %copy.96), kind=kLoop, calls=%fused_computation.26 | loop fusion | flops 786432 | bytes 3146752 | tf_op jit(solution)/shard_map/reduce_sum | solution.py:92
  307.5 3.4 %collective-permute-start = (bf16[128,2048]{1,0:T(8,128)(2,1)S(1)}, bf16[128,2048]{1,0:T(8,128)(2,1)S(1)}, u32[]{:S(2)}, u32[]{:S(2)}) collective-permute-start(bf16[128,2048]{1,0:T(8,128)(2,1)S(1)} %fusion.61), channel_id=1, source_target_pairs={{0,8},{8,16},{16,24},{1,9},{9,17},{17,25},{2,10},{10,18},{18,26},{... | collective-permute-start | bytes 1572872 | tf_op jit(solution)/shard_map/ppermute | solution.py:14
  310.9 6.5 %psum.55 = f32[1,2048]{1,0:T(1,128)} all-reduce(f32[1,2048]{1,0:T(1,128)S(1)} %bitcast.277), channel_id=1, replica_groups=mesh['pipe'=4,'dp'=4,'expert'=2] {'dp'}, use_global_device_ids=true, to_apply=%region_27.29 | all-reduce | flops 2048 | bytes 16384 | tf_op jit(solution)/shard_map/psum | solution.py:200
  317.4 0.9 fusion.64
  318.3 3.6 %collective-permute-done = bf16[128,2048]{1,0:T(8,128)(2,1)S(1)} collective-permute-done((bf16[128,2048]{1,0:T(8,128)(2,1)S(1)}, bf16[128,2048]{1,0:T(8,128)(2,1)S(1)}, u32[]{:S(2)}, u32[]{:S(2)}) %collective-permute-start) | collective-permute-done | bytes 524320 | tf_op jit(solution)/shard_map/ppermute | solution.py:14
  321.9 0.8 copy.151
  322.7 1.9 copy.152
  (75 shorter events, 2.4 us)
Async XLA Ops:
  7.2 114.1 %copy-start = (bf16[1,2048,4]{1,2,0:T(4,128)(2,1)S(1)}, bf16[1,2048,4]{1,2,0:T(4,128)(2,1)}, u32[]{:S(2)}) copy-start(bf16[1,2048,4]{1,2,0:T(4,128)(2,1)} %param.17) | copy-start | bytes 49156
  7.2 64.6 %all-gather.8.cloned.1.call-start = ((), (), s32[]{:S(2)}) async-start(), calls=%async_computation.11 | async-start | bytes 3145728 | tf_op jit(solution)/shard_map/all_gather | solution.py:113
  20.0 17.8 %copy-start.3 = (bf16[1,128,2048]{2,1,0:T(8,128)(2,1)S(1)}, bf16[1,128,2048]{2,1,0:T(8,128)(2,1)}, u32[]{:S(2)}) copy-start(bf16[1,128,2048]{2,1,0:T(8,128)(2,1)} %param.12) | copy-start | bytes 1572868
  37.8 68.7 %all-gather.6.cloned.1.call-start = ((), (), s32[]{:S(2)}) async-start(), calls=%async_computation.10 | async-start | bytes 3145728 | tf_op jit(solution)/shard_map/all_gather | solution.py:114
  57.1 93.4 %reduce-scatter.5.cloned.1.call-start = ((), (), s32[]{:S(2)}) async-start(), calls=%async_computation.12 | async-start | bytes 3145728 | tf_op jit(solution)/shard_map/reduce_scatter | solution.py:137
  118.0 0.7 copy-start.8
  118.0 1.1 copy-start.7
  118.0 3.1 copy-start.1
  118.0 3.3 copy-start.2
  118.0 3.3 %copy-start.6 = (f32[1,2048]{1,0:T(1,128)S(1)}, f32[1,2048]{1,0:T(1,128)}, u32[]{:S(2)}) copy-start(f32[1,2048]{1,0:T(1,128)} %param.16) | copy-start | bytes 24580
  129.7 6.9 %all-to-all-start.5 = ((bf16[4,1,64]{2,1,0:T(2,128)(2,1)}), bf16[4,1,64]{2,1,0:T(2,128)(2,1)S(1)}, u32[]{:S(2)}, u32[]{:S(2)}) async-start(bf16[4,1,64]{2,1,0:T(2,128)(2,1)} %get-tuple-element.14), calls=%async_computation.7 | async-start | bytes 4096 | tf_op jit(solution)/shard_map/all_to_all | solution.py:142
  150.5 17.9 %all-to-all-start.4 = ((bf16[4,1,64,2048]{3,2,1,0:T(8,128)(2,1)}), bf16[4,1,64,2048]{3,2,1,0:T(8,128)(2,1)S(1)}, u32[]{:S(2)}, u32[]{:S(2)}) async-start(bf16[4,1,64,2048]{3,2,1,0:T(8,128)(2,1)} %bitcast.265), calls=%async_computation.6 | async-start | bytes 2097152 | tf_op jit(solution)/shard_map/all_to_all | solution.py:141
  154.0 83.4 %all-gather.4.cloned.1.call-start = ((), (), s32[]{:S(2)}) async-start(), calls=%async_computation.8 | async-start | bytes 3145728 | tf_op jit(solution)/shard_map/all_gather | solution.py:76
  174.5 10.8 %copy-start.4 = (bf16[1,128,2048]{2,1,0:T(8,128)(2,1)S(1)}, bf16[1,128,2048]{2,1,0:T(8,128)(2,1)}, u32[]{:S(2)}) copy-start(bf16[1,128,2048]{2,1,0:T(8,128)(2,1)} %param.12) | copy-start | bytes 1572868
  185.7 96.6 %copy-start.5 = (bf16[128,2048]{1,0:T(8,128)(2,1)}, bf16[128,2048]{1,0:T(8,128)(2,1)S(1)}, u32[]{:S(2)}) copy-start(bf16[128,2048]{1,0:T(8,128)(2,1)S(1)} %get-tuple-element.26) | copy-start | bytes 1572868
  205.0 73.6 %reduce-scatter.3.cloned.1.call-start = ((), (), s32[]{:S(2)}) async-start(), calls=%async_computation.9 | async-start | bytes 3145728 | tf_op jit(solution)/shard_map/reduce_scatter | solution.py:83
  237.4 6.5 %copy-start.9 = (bf16[1,1,512,4096]{3,2,1,0:T(8,128)(2,1)S(1)}, bf16[1,1,512,4096]{3,2,1,0:T(8,128)(2,1)}, u32[]{:S(2)}) copy-start(bf16[1,1,512,4096]{3,2,1,0:T(8,128)(2,1)} %param.19) | copy-start | bytes 12582916
  278.6 17.9 %all-to-all-start.1 = ((bf16[4,1,64,2048]{3,2,1,0:T(8,128)(2,1)}), bf16[4,1,64,2048]{3,2,1,0:T(8,128)(2,1)S(1)}, u32[]{:S(2)}, u32[]{:S(2)}) async-start(bf16[4,1,64,2048]{3,2,1,0:T(8,128)(2,1)} %bitcast.266), calls=%async_computation.2 | async-start | bytes 2097152 | tf_op jit(solution)/shard_map/all_to_all | solution.py:86
  282.4 35.0 %collective-permute-start.1 = (bf16[128,2048]{1,0:T(8,128)(2,1)S(1)}, bf16[128,2048]{1,0:T(8,128)(2,1)}, u32[]{:S(2)}, u32[]{:S(2)}) collective-permute-start(bf16[128,2048]{1,0:T(8,128)(2,1)S(1)} %get-tuple-element.26), channel_id=1, source_target_pairs={{8,0},{16,8},{24,16},{9,1},{17,9},{25,17},{10,2},{18,10},{26,18},{... | collective-permute-start | bytes 1572872 | tf_op jit(solution)/shard_map/ppermute | solution.py:14
  307.5 14.4 %collective-permute-start = (bf16[128,2048]{1,0:T(8,128)(2,1)S(1)}, bf16[128,2048]{1,0:T(8,128)(2,1)S(1)}, u32[]{:S(2)}, u32[]{:S(2)}) collective-permute-start(bf16[128,2048]{1,0:T(8,128)(2,1)S(1)} %fusion.61), channel_id=1, source_target_pairs={{0,8},{8,16},{16,24},{1,9},{9,17},{17,25},{2,10},{10,18},{18,26},{... | collective-permute-start | bytes 1572872 | tf_op jit(solution)/shard_map/ppermute | solution.py:14
Sparse Core Ops, SparseCore 0:
  37.9 33.8 all-gather.7
  73.3 33.0 all-gather.5
  118.1 32.2 reduce-scatter.4
  205.1 32.1 all-gather.3
  246.7 31.8 reduce-scatter.2
where the time goes:
time: 332 us; the launch traced here: 331 us
  waiting for transfers between devices  153 us (46%)
  blocking collectives  78.3 us (24%)
  matrix products  30.2 us (9%)
  local copies, waits for them, and re-layouts  20.6 us (6%)
  other arithmetic  19.6 us (6%)
  starting transfers between devices  15.6 us (5%)
  between operations  14.2 us (4%)
    reduce_scatter x2, waiting for transfers between devices, compute(): lax.psum_scatter(partial_value.astype(jnp.bfloat16), 'expert', scatter_di...  45.9 us
    all_gather x1, waiting for transfers between devices, compute(): lax.all_gather(received, 'expert', axis=3, tiled=True)  32.3 us
    all_gather x1, waiting for transfers between devices, compute(): up_piece = lax.all_gather(up_in, 'expert', axis=3, tiled=True)  28.3 us
    psum x3, blocking collectives, feature_sum(): return lax.psum(values, 'expert')  18.9 us
    all_to_all x1, blocking collectives, run_backward(): lax.all_to_all(row_buffer, 'dp', split_axis=0, concat_axis=0, tiled=True)  17.7 us
    all_to_all x1, blocking collectives, run_forward(): lax.all_to_all(buffer, 'dp', split_axis=0, concat_axis=0, tiled=True)  17.6 us
    all_to_all x1, blocking collectives, run_backward(): lax.all_to_all(upstream_buffer, 'dp', split_axis=0, concat_axis=0, tiled=...  17.6 us
    all_gather x1, waiting for transfers between devices, compute(): rows_piece = lax.all_gather(rows_in, 'expert', axis=3, tiled=True)  14.7 us
  transfers between devices with their start and end apart: 10, of which 9 were waited for; matrix products, arithmetic and copies ran while one was open for 8% of the time, Pallas kernels for 0%

commit v1 on v0

--- a/solution.py
+++ b/solution.py
@@ -6,6 +6,24 @@
 D = 4096
 ROUTE_SCALE = 2.827
 EPSILON = 1e-05
+
+
+def chains_treat(frame, peer_axis, m):
+    w_next = lax.axis_size(peer_axis)
+    out_arr = lax.axis_index(peer_axis)
+    next_value, r2, clean = (w_next, out_arr, frame.shape[3])
+    a_next = range(next_value)
+    upper = map(lambda ii: (ii, (ii + 1) % next_value), a_next)
+    samples = list(upper)
+    main, plain = (frame, None)
+    for p in range(next_value):
+        block_last = (
+            lax.ppermute(main, perm=samples, axis_name=peer_axis) if p < next_value - 1 else None
+        )
+        back = m(main, (r2 - p) % next_value * clean)
+        plain = back if plain is None else plain + back
+        main = block_last
+    return plain
 
 
 def shifted(block, axis, distance):
@@ -111,12 +129,18 @@
     def compute(received):
         rows_in, up_in = received
         rows_piece = lax.all_gather(rows_in, "expert", axis=3, tiled=True)
-        up_piece = lax.all_gather(up_in, "expert", axis=3, tiled=True)
         first_sum = jnp.einsum(
             "sxcd,xdkf->sxckf", rows_piece, gate_up, preferred_element_type=jnp.float32
         )
-        second_sum = jnp.einsum(
-            "sxcd,xfd->sxcf", up_piece, down_w, preferred_element_type=jnp.float32
+        second_sum = chains_treat(
+            up_in,
+            "expert",
+            lambda shard, start: jnp.einsum(
+                "sxcd,xfd->sxcf",
+                shard,
+                lax.dynamic_slice_in_dim(down_w, start, shard.shape[3], axis=2),
+                preferred_element_type=jnp.float32,
+            ),
         )
         gate_pre = first_sum[:, :, :, 0]
         second = first_sum[:, :, :, 1]

time: 332 us -> 316 us (0.952)
  waiting for transfers between devices: 153 us -> 136 us
    all_gather x1 -> x0, waiting for transfers between devices: 28.3 us -> none  [compute(): up_piece = lax.all_gather(up_in, 'expert', axis=3, tiled=True)]
    all_gather x1, waiting for transfers between devices: 14.7 us -> 23.7 us  [compute(): rows_piece = lax.all_gather(rows_in, 'expert', axis=3, tiled=True)]
  transfers between devices with their start and end apart: 10 -> 10, of which waited for: 9 -> 9; matrix products, arithmetic and copies ran while one was open for 8% -> 9% of each run, Pallas kernels for 0% -> 0%
where the time goes in v1:
time: 316 us; the launch traced here: 315 us
  waiting for transfers between devices  136 us (43%)
  blocking collectives  77.6 us (25%)
  matrix products  29.5 us (9%)
  local copies, waits for them, and re-layouts  20.6 us (7%)
  other arithmetic  19.6 us (6%)
  starting transfers between devices  17.6 us (6%)
  between operations  14.2 us (4%)
    reduce_scatter x2, waiting for transfers between devices, compute(): lax.psum_scatter(partial_value.astype(jnp.bfloat16), 'expert', scatter_di...  45.9 us
    all_gather x1, waiting for transfers between devices, compute(): lax.all_gather(received, 'expert', axis=3, tiled=True)  32.3 us
    all_gather x1, waiting for transfers between devices, compute(): rows_piece = lax.all_gather(rows_in, 'expert', axis=3, tiled=True)  23.7 us
    psum x3, blocking collectives, feature_sum(): return lax.psum(values, 'expert')  18.9 us
    all_to_all x1, blocking collectives, run_backward(): lax.all_to_all(row_buffer, 'dp', split_axis=0, concat_axis=0, tiled=True)  17.7 us
    all_to_all x1, blocking collectives, run_forward(): lax.all_to_all(buffer, 'dp', split_axis=0, concat_axis=0, tiled=True)  17.6 us
    all_to_all x1, blocking collectives, run_backward(): lax.all_to_all(upstream_buffer, 'dp', split_axis=0, concat_axis=0, tiled=...  16.9 us
    all_to_all x1, waiting for transfers between devices, compute(): return lax.all_to_all(summed, 'dp', split_axis=0, concat_axis=0, tiled=True)  12.7 us
  transfers between devices with their start and end apart: 10, of which 9 were waited for; matrix products, arithmetic and copies ran while one was open for 9% of the time, Pallas kernels for 0%

profile of v1, /device:TPU:0, one launch (start us, length us, event | category | flops | bytes accessed | tf_op | source)
XLA Modules:
  0.0 315.4 jit_solution(7872391133897873411)
XLA Ops:
  7.2 0.8 copy.106
  8.2 0.1 reshape_squeeze.7
  8.3 1.2 fusion.50
  9.5 5.9 %psum.51 = f32[128,1]{0,1:T(1,128)S(1)} all-reduce(f32[128,1]{0,1:T(1,128)S(1)} %bitcast.293), channel_id=1, replica_groups=mesh['pipe'=4,'dp'=4,'expert'=2] {'expert'}, use_global_device_ids=true, to_apply=%region_11.13 | all-reduce | flops 128 | bytes 1024 | tf_op jit(solution)/shard_map/psum | solution.py:36
  15.4 1.2 fusion.52
  16.7 0.6 broadcast_in_dim.66
  17.3 0.4 reshape.451
  17.8 1.2 reduce-window.16
  19.4 0.6 convolution_convert_fusion.1
  20.0 17.7 %all_to_all.30 = bf16[4,1,64,2048]{3,2,1,0:T(8,128)(2,1)} all-to-all(bf16[4,1,64,2048]{3,2,1,0:T(8,128)(2,1)S(1)} %bitcast.269), channel_id=1, replica_groups=mesh['pipe'=4,'dp'=4,'expert'=2] {'dp'}, dimensions={0} | all-to-all | bytes 2097152 | tf_op jit(solution)/shard_map/all_to_all | solution.py:171
  37.8 0.6 broadcast_in_dim.65
  38.5 0.4 reshape.446
  38.9 0.6 convolution_convert_fusion.2
  39.5 16.9 %all_to_all.31 = bf16[4,1,64,2048]{3,2,1,0:T(8,128)(2,1)S(1)} all-to-all(bf16[4,1,64,2048]{3,2,1,0:T(8,128)(2,1)S(1)} %bitcast.270), channel_id=1, replica_groups=mesh['pipe'=4,'dp'=4,'expert'=2] {'dp'}, dimensions={0} | all-to-all | bytes 2097152 | tf_op jit(solution)/shard_map/all_to_all | solution.py:172
  56.3 2.0 collective-permute-start
  58.3 2.3 fusion.20
  60.7 23.7 %all-gather.5.cloned.1.call-done = bf16[4,1,64,4096]{3,2,0,1:T(8,128)(2,1)} async-done(((bf16[4,1,64,2048]{3,2,0,1:T(8,128)(2,1)}), bf16[4,1,64,4096]{3,2,0,1:T(8,128)(2,1)}) %all-gather.5.cloned.1.call-update) | async-done | bytes 2097168 | tf_op jit(solution)/shard_map/all_gather | solution.py:131
  84.3 6.5 %fusion.29 = f32[4,1,64,2,512]{4,2,0,3,1:T(8,128)S(1)} fusion(bf16[4096,2,512,1]{2,1,0,3:T(2,128)(2,1)} %bitcast.294, bf16[4,1,64,4096]{3,2,0,1:T(8,128)(2,1)} %all-gather.5.cloned.1.call-done), kind=kOutput, calls=%fused_computation.36 | convolution fusion | flops 2147483648 | bytes 11534336 | tf_op jit(solution)/shard_map/sxcd,xdkf->sxckf/dot_general | solution.py:132
  90.8 3.2 %collective-permute-done = bf16[4,1,64,2048]{3,2,0,1:T(8,128)(2,1)S(1)} collective-permute-done((bf16[4,1,64,2048]{3,2,0,1:T(8,128)(2,1)S(1)}, bf16[4,1,64,2048]{3,2,0,1:T(8,128)(2,1)S(1)}, u32[]{:S(2)}, u32[]{:S(2)}) %collective-permute-start) | collective-permute-done | bytes 1048608 | tf_op jit(solution)/shard_map/ppermute | solution.py:21
  94.1 1.2 fusion.88
  95.2 7.1 %fusion.14 = bf16[4,1,64,4096]{3,2,0,1:T(8,128)(2,1)} fusion(bf16[4096,2,512,1]{2,1,0,3:T(2,128)(2,1)} %bitcast.295, bf16[4,1,64,1,512]{4,2,0,3,1:T(8,128)(2,1)S(1)} %get-tuple-element.25, bf16[4,1,64,1,512]{4,2,0,3,1:T(8,128)(2,1)S(1)} %get-tuple-element.23), kind=kOutput, calls=%fused_computation.14 | convolution fusion | flops 2148794368 | bytes 11010048 | tf_op jit(solution)/shard_map/sxckf,xdkf->sxcd/dot_general | solution.py:158
  102.5 0.5 copy-done.8
  103.3 0.1 reshape_squeeze.6
  103.7 1.2 reduce-window.14
  105.4 0.2 fusion.62
  105.7 0.3 fusion.75
  106.0 8.1 %all-reduce.1 = (f32[128,1]{0,1:T(1,128)S(1)}, f32[128,4]{0,1:T(4,128)S(1)}, bf16[4,1,64]{2,1,0:T(2,128)(2,1)}) all-reduce(f32[128,1]{0,1:T(1,128)S(1)} %bitcast.291, f32[128,4]{0,1:T(4,128)S(1)} %fusion.75, f32[4,1,64]{2,1,0:T(1,128)S(1)} %bitcast.292), channel_id=1, replica_groups=mesh['pipe'=4,'dp'=4,'expert'=2] {'expert'}, use_global_device_ids=true, to_apply=%region_1.0 | all-reduce | flops 896 | bytes 6656 | tf_op jit(solution)/shard_map/psum | solution.py:36
  114.1 3.2 %all-to-all-start.5 = ((bf16[4,1,64]{2,1,0:T(2,128)(2,1)}), bf16[4,1,64]{2,1,0:T(2,128)(2,1)S(1)}, u32[]{:S(2)}, u32[]{:S(2)}) async-start(bf16[4,1,64]{2,1,0:T(2,128)(2,1)} %get-tuple-element.14), calls=%async_computation.7 | async-start | bytes 4096 | tf_op jit(solution)/shard_map/all_to_all | solution.py:166
  117.3 3.6 %all-to-all-done.5 = bf16[4,1,64]{2,1,0:T(2,128)(2,1)S(1)} async-done(((bf16[4,1,64]{2,1,0:T(2,128)(2,1)}), bf16[4,1,64]{2,1,0:T(2,128)(2,1)S(1)}, u32[]{:S(2)}, u32[]{:S(2)}) %all-to-all-start.5) | async-done | bytes 544 | tf_op jit(solution)/shard_map/all_to_all | solution.py:166
  121.0 13.9 %reduce-scatter.5.cloned.1.call-done = bf16[4,1,64,2048]{3,2,0,1:T(8,128)(2,1)} async-done(((bf16[4,1,64,4096]{3,2,0,1:T(8,128)(2,1)}), bf16[4,1,64,2048]{3,2,0,1:T(8,128)(2,1)}) %reduce-scatter.5.cloned.1.call-update) | async-done | bytes 1048592 | tf_op jit(solution)/shard_map/reduce_scatter | solution.py:161
  134.8 3.5 %all-to-all-start.4 = ((bf16[4,1,64,2048]{3,2,1,0:T(8,128)(2,1)}), bf16[4,1,64,2048]{3,2,1,0:T(8,128)(2,1)S(1)}, u32[]{:S(2)}, u32[]{:S(2)}) async-start(bf16[4,1,64,2048]{3,2,1,0:T(8,128)(2,1)} %bitcast.273), calls=%async_computation.6 | async-start | bytes 2097152 | tf_op jit(solution)/shard_map/all_to_all | solution.py:165
  138.4 0.2 all-gather.3.cloned.1.call-start
  138.6 0.3 fusion.72
  139.0 1.9 gather_fusion
  140.9 0.2 gather.10
  141.3 11.4 %all-to-all-done.4 = bf16[4,1,64,2048]{3,2,1,0:T(8,128)(2,1)S(1)} async-done(((bf16[4,1,64,2048]{3,2,1,0:T(8,128)(2,1)}), bf16[4,1,64,2048]{3,2,1,0:T(8,128)(2,1)S(1)}, u32[]{:S(2)}, u32[]{:S(2)}) %all-to-all-start.4) | async-done | bytes 1048608 | tf_op jit(solution)/shard_map/all_to_all | solution.py:165
  152.8 2.3 gather_fusion.2
  155.1 1.4 select_convert_fusion
  156.5 2.3 reshape.461
  158.9 4.8 %multiply_reduce_fusion = bf16[128,2048]{1,0:T(8,128)(2,1)S(1)} fusion(f32[128,2,2048]{2,1,0:T(2,128)} %reshape.461, f32[128,2]{1,0:T(8,128)S(1)} %copy.105), kind=kLoop, calls=%fused_computation.26 | loop fusion | flops 786432 | bytes 2622464 | tf_op jit(solution)/shard_map/reduce_sum | solution.py:183
  163.7 1.0 fusion.59
  164.7 4.9 %all-reduce = (f32[128,4]{0,1:T(4,128)S(1)}, f32[128]{0:T(128)S(1)}) all-reduce(f32[128,4]{0,1:T(4,128)S(1)} %fusion.72, f32[128]{0:T(128)S(1)} %get-tuple-element.7), channel_id=1, replica_groups=mesh['pipe'=4,'dp'=4,'expert'=2] {'expert'}, use_global_device_ids=true, to_apply=%region_2.0 | all-reduce | flops 640 | bytes 5120 | tf_op jit(solution)/shard_map/psum | solution.py:36
  169.6 0.5 fusion.56
  170.1 0.6 broadcast_in_dim.36
  170.8 0.4 reshape.438
  171.2 0.6 convolution_convert_fusion.3
  171.8 17.6 %all_to_all.32 = bf16[4,1,64,2048]{3,2,1,0:T(8,128)(2,1)} all-to-all(bf16[4,1,64,2048]{3,2,1,0:T(8,128)(2,1)S(1)} %bitcast.271), channel_id=1, replica_groups=mesh['pipe'=4,'dp'=4,'expert'=2] {'dp'}, dimensions={0} | all-to-all | bytes 2097152 | tf_op jit(solution)/shard_map/all_to_all | solution.py:106
  189.5 32.3 %all-gather.3.cloned.1.call-done = bf16[4,1,64,4096]{3,2,0,1:T(8,128)(2,1)} async-done(((bf16[4,1,64,2048]{3,2,0,1:T(8,128)(2,1)}), bf16[4,1,64,4096]{3,2,0,1:T(8,128)(2,1)}) %all-gather.3.cloned.1.call-update) | async-done | bytes 2097168 | tf_op jit(solution)/shard_map/all_gather | solution.py:94
  221.8 6.5 %fusion.34 = f32[4,1,64,2,512]{4,2,3,0,1:T(8,128)S(1)} fusion(bf16[4096,2,512]{2,1,0:T(2,128)(2,1)} %bitcast.296, bf16[4,1,64,4096]{3,2,0,1:T(8,128)(2,1)} %all-gather.3.cloned.1.call-done), kind=kOutput, calls=%fused_computation.37 | convolution fusion | flops 2147483648 | bytes 11534336 | tf_op jit(solution)/shard_map/sxcd,xdkf->sxckf/dot_general | solution.py:78
  228.3 2.7 fusion.13
  230.9 32.1 %reduce-scatter.3.cloned.1.call-done = bf16[4,1,64,2048]{3,2,0,1:T(8,128)(2,1)} async-done(((bf16[4,1,64,4096]{3,2,0,1:T(8,128)(2,1)}), bf16[4,1,64,2048]{3,2,0,1:T(8,128)(2,1)}) %reduce-scatter.3.cloned.1.call-update) | async-done | bytes 1048592 | tf_op jit(solution)/shard_map/reduce_scatter | solution.py:101
  263.0 3.5 %all-to-all-start.1 = ((bf16[4,1,64,2048]{3,2,1,0:T(8,128)(2,1)}), bf16[4,1,64,2048]{3,2,1,0:T(8,128)(2,1)S(1)}, u32[]{:S(2)}, u32[]{:S(2)}) async-start(bf16[4,1,64,2048]{3,2,1,0:T(8,128)(2,1)} %bitcast.275), calls=%async_computation.2 | async-start | bytes 2097152 | tf_op jit(solution)/shard_map/all_to_all | solution.py:104
  266.7 1.5 collective-permute-start.2
  268.3 12.7 %all-to-all-done.1 = bf16[4,1,64,2048]{3,2,1,0:T(8,128)(2,1)S(1)} async-done(((bf16[4,1,64,2048]{3,2,1,0:T(8,128)(2,1)}), bf16[4,1,64,2048]{3,2,1,0:T(8,128)(2,1)S(1)}, u32[]{:S(2)}, u32[]{:S(2)}) %all-to-all-start.1) | async-done | bytes 1048608 | tf_op jit(solution)/shard_map/all_to_all | solution.py:104
  280.9 2.3 gather_fusion.1
  283.3 1.4 select_convert_fusion.1
  284.7 2.3 reshape.459
  287.0 4.7 %multiply_reduce_fusion.1 = f32[128,2048]{1,0:T(8,128)S(1)} fusion(f32[128,2,2048]{2,1,0:T(2,128)} %reshape.459, f32[128,2]{1,0:T(8,128)S(1)} %copy.96), kind=kLoop, calls=%fused_computation.29 | loop fusion | flops 786432 | bytes 3146752 | tf_op jit(solution)/shard_map/reduce_sum | solution.py:110
  291.9 3.4 %collective-permute-start.1 = (bf16[128,2048]{1,0:T(8,128)(2,1)S(1)}, bf16[128,2048]{1,0:T(8,128)(2,1)S(1)}, u32[]{:S(2)}, u32[]{:S(2)}) collective-permute-start(bf16[128,2048]{1,0:T(8,128)(2,1)S(1)} %fusion.65), channel_id=1, source_target_pairs={{0,8},{8,16},{16,24},{1,9},{9,17},{17,25},{2,10},{10,18},{18,26},{... | collective-permute-start | bytes 1572872 | tf_op jit(solution)/shard_map/ppermute | solution.py:32
  295.3 6.5 %psum.55 = f32[1,2048]{1,0:T(1,128)} all-reduce(f32[1,2048]{1,0:T(1,128)S(1)} %bitcast.286), channel_id=1, replica_groups=mesh['pipe'=4,'dp'=4,'expert'=2] {'dp'}, use_global_device_ids=true, to_apply=%region_27.29 | all-reduce | flops 2048 | bytes 16384 | tf_op jit(solution)/shard_map/psum | solution.py:224
  301.8 0.9 fusion.68
  302.7 3.6 %collective-permute-done.1 = bf16[128,2048]{1,0:T(8,128)(2,1)S(1)} collective-permute-done((bf16[128,2048]{1,0:T(8,128)(2,1)S(1)}, bf16[128,2048]{1,0:T(8,128)(2,1)S(1)}, u32[]{:S(2)}, u32[]{:S(2)}) %collective-permute-start.1) | collective-permute-done | bytes 524320 | tf_op jit(solution)/shard_map/ppermute | solution.py:32
  306.2 0.8 copy.151
  307.0 1.9 copy.152
  (77 shorter events, 2.7 us)
Async XLA Ops:
  7.2 98.5 %copy-start = (bf16[1,2048,4]{1,2,0:T(4,128)(2,1)S(1)}, bf16[1,2048,4]{1,2,0:T(4,128)(2,1)}, u32[]{:S(2)}) copy-start(bf16[1,2048,4]{1,2,0:T(4,128)(2,1)} %param.17) | copy-start | bytes 49156
  7.2 77.2 %all-gather.5.cloned.1.call-start = ((), (), s32[]{:S(2)}) async-start(), calls=%async_computation.10 | async-start | bytes 3145728 | tf_op jit(solution)/shard_map/all_gather | solution.py:131
  20.0 17.8 %copy-start.3 = (bf16[1,128,2048]{2,1,0:T(8,128)(2,1)S(1)}, bf16[1,128,2048]{2,1,0:T(8,128)(2,1)}, u32[]{:S(2)}) copy-start(bf16[1,128,2048]{2,1,0:T(8,128)(2,1)} %param.12) | copy-start | bytes 1572868
  37.8 97.1 %reduce-scatter.5.cloned.1.call-start = ((), (), s32[]{:S(2)}) async-start(), calls=%async_computation.11 | async-start | bytes 3145728 | tf_op jit(solution)/shard_map/reduce_scatter | solution.py:161
  56.3 37.7 %collective-permute-start = (bf16[4,1,64,2048]{3,2,0,1:T(8,128)(2,1)S(1)}, bf16[4,1,64,2048]{3,2,0,1:T(8,128)(2,1)S(1)}, u32[]{:S(2)}, u32[]{:S(2)}) collective-permute-start(bf16[4,1,64,2048]{3,2,0,1:T(8,128)(2,1)S(1)} %bitcast.274), channel_id=1, source_target_pairs={{0,1},{1,0},{2,3},{3,2},{4,5},{5,4},{6,7},{7,6},{8,9},{9,8},{10,11... | collective-permute-start | bytes 3145736 | tf_op jit(solution)/shard_map/ppermute | solution.py:21
  84.3 9.7 %copy-start.9 = (bf16[1,1,512,4096]{3,2,1,0:T(8,128)(2,1)S(1)}, bf16[1,1,512,4096]{3,2,1,0:T(8,128)(2,1)}, u32[]{:S(2)}) copy-start(bf16[1,1,512,4096]{3,2,1,0:T(8,128)(2,1)} %param.19) | copy-start | bytes 12582916
  102.3 0.7 copy-start.8
  102.3 1.1 copy-start.7
  102.3 3.1 copy-start.1
  102.3 3.3 %copy-start.2 = (bf16[1,128,2048]{2,1,0:T(8,128)(2,1)S(1)}, bf16[1,128,2048]{2,1,0:T(8,128)(2,1)}, u32[]{:S(2)}) copy-start(bf16[1,128,2048]{2,1,0:T(8,128)(2,1)} %param.13) | copy-start | bytes 1572868
  102.3 3.3 %copy-start.6 = (f32[1,2048]{1,0:T(1,128)S(1)}, f32[1,2048]{1,0:T(1,128)}, u32[]{:S(2)}) copy-start(f32[1,2048]{1,0:T(1,128)} %param.16) | copy-start | bytes 24580
  114.1 6.9 %all-to-all-start.5 = ((bf16[4,1,64]{2,1,0:T(2,128)(2,1)}), bf16[4,1,64]{2,1,0:T(2,128)(2,1)S(1)}, u32[]{:S(2)}, u32[]{:S(2)}) async-start(bf16[4,1,64]{2,1,0:T(2,128)(2,1)} %get-tuple-element.14), calls=%async_computation.7 | async-start | bytes 4096 | tf_op jit(solution)/shard_map/all_to_all | solution.py:166
  134.8 17.9 %all-to-all-start.4 = ((bf16[4,1,64,2048]{3,2,1,0:T(8,128)(2,1)}), bf16[4,1,64,2048]{3,2,1,0:T(8,128)(2,1)S(1)}, u32[]{:S(2)}, u32[]{:S(2)}) async-start(bf16[4,1,64,2048]{3,2,1,0:T(8,128)(2,1)} %bitcast.273), calls=%async_computation.6 | async-start | bytes 2097152 | tf_op jit(solution)/shard_map/all_to_all | solution.py:165
  138.4 83.4 %all-gather.3.cloned.1.call-start = ((), (), s32[]{:S(2)}) async-start(), calls=%async_computation.8 | async-start | bytes 3145728 | tf_op jit(solution)/shard_map/all_gather | solution.py:94
  158.8 10.8 %copy-start.4 = (bf16[1,128,2048]{2,1,0:T(8,128)(2,1)S(1)}, bf16[1,128,2048]{2,1,0:T(8,128)(2,1)}, u32[]{:S(2)}) copy-start(bf16[1,128,2048]{2,1,0:T(8,128)(2,1)} %param.12) | copy-start | bytes 1572868
  170.1 96.6 %copy-start.5 = (bf16[128,2048]{1,0:T(8,128)(2,1)}, bf16[128,2048]{1,0:T(8,128)(2,1)S(1)}, u32[]{:S(2)}) copy-start(bf16[128,2048]{1,0:T(8,128)(2,1)S(1)} %get-tuple-element.26) | copy-start | bytes 1572868
  189.4 73.6 %reduce-scatter.3.cloned.1.call-start = ((), (), s32[]{:S(2)}) async-start(), calls=%async_computation.9 | async-start | bytes 3145728 | tf_op jit(solution)/shard_map/reduce_scatter | solution.py:101
  221.8 6.5 %copy-start.10 = (bf16[1,1,512,4096]{3,2,1,0:T(8,128)(2,1)S(1)}, bf16[1,1,512,4096]{3,2,1,0:T(8,128)(2,1)}, u32[]{:S(2)}) copy-start(bf16[1,1,512,4096]{3,2,1,0:T(8,128)(2,1)} %param.19) | copy-start | bytes 12582916
  263.0 17.9 %all-to-all-start.1 = ((bf16[4,1,64,2048]{3,2,1,0:T(8,128)(2,1)}), bf16[4,1,64,2048]{3,2,1,0:T(8,128)(2,1)S(1)}, u32[]{:S(2)}, u32[]{:S(2)}) async-start(bf16[4,1,64,2048]{3,2,1,0:T(8,128)(2,1)} %bitcast.275), calls=%async_computation.2 | async-start | bytes 2097152 | tf_op jit(solution)/shard_map/all_to_all | solution.py:104
  266.7 35.0 %collective-permute-start.2 = (bf16[128,2048]{1,0:T(8,128)(2,1)S(1)}, bf16[128,2048]{1,0:T(8,128)(2,1)}, u32[]{:S(2)}, u32[]{:S(2)}) collective-permute-start(bf16[128,2048]{1,0:T(8,128)(2,1)S(1)} %get-tuple-element.26), channel_id=1, source_target_pairs={{8,0},{16,8},{24,16},{9,1},{17,9},{25,17},{10,2},{18,10},{26,18},{... | collective-permute-start | bytes 1572872 | tf_op jit(solution)/shard_map/ppermute | solution.py:32
  291.9 14.4 %collective-permute-start.1 = (bf16[128,2048]{1,0:T(8,128)(2,1)S(1)}, bf16[128,2048]{1,0:T(8,128)(2,1)S(1)}, u32[]{:S(2)}, u32[]{:S(2)}) collective-permute-start(bf16[128,2048]{1,0:T(8,128)(2,1)S(1)} %fusion.65), channel_id=1, source_target_pairs={{0,8},{8,16},{16,24},{1,9},{9,17},{17,25},{2,10},{10,18},{18,26},{... | collective-permute-start | bytes 1572872 | tf_op jit(solution)/shard_map/ppermute | solution.py:32
Sparse Core Ops, SparseCore 0:
  37.9 46.4 all-gather.4
  102.5 32.2 reduce-scatter.4
  189.5 32.1 all-gather.2
  231.1 31.8 reduce-scatter.2
